TPU v7x, 256 devices: a whole 4x4x8 slice. The times are simulated.
256 devices in a mesh: dp: 4 (over y_lo, core), sp: 8 (over y_hi, x), tp: 8 (over z).
Axes of the slice: x: 4, y: 4 (y_hi: 2, y_lo: 2; y = y_hi * 2 + y_lo), z: 8, core: 2. Of those that a mesh axis runs over, the one named last changes fastest.
Arguments:
- query: bfloat16 [4, 3072, 3072], P('dp', 'sp', 'tp'), may hold values from -110 to 110
- key: bfloat16 [4, 3072, 3072], P('dp', 'sp', 'tp'), may hold values from -8 to 8
- value: bfloat16 [4, 3072, 3072], P('dp', 'sp', 'tp'), may hold values from -6 to 6
- text_key: bfloat16 [4, 256, 3072], P('dp', None, 'tp'), may hold values from -6 to 6
- text_value: bfloat16 [4, 256, 3072], P('dp', None, 'tp'), may hold values from -6 to 6
- grad_out: bfloat16 [4, 3072, 3072], P('dp', 'sp', 'tp'), may hold values from -6 to 6
- gate: bfloat16 [4, 3072], P('dp'), may hold values from 0.5 to 1.5
- out_weight: bfloat16 [3072, 3072], P('tp', 'dp'), may hold values from -0.109375 to 0.109375
- windows: int32 [8, 2], P('sp'), may hold values from 0 to 2, as said below
- tile_map: int32 [8, 1], replicated, may hold values from 0 to 2, as said below
- text_count: int32 [4], P('dp'), may hold values from 1 to 256
Outputs:
- grad_query: bfloat16 [4, 3072, 3072], P('dp', 'sp', 'tp')
- grad_key: bfloat16 [4, 3072, 3072], P('dp', 'sp', 'tp')
- grad_value: bfloat16 [4, 3072, 3072], P('dp', 'sp', 'tp')
- grad_text_key: bfloat16 [4, 256, 3072], P('dp', None, 'tp')
- grad_text_value: bfloat16 [4, 256, 3072], P('dp', None, 'tp')
- grad_weight: float32 [3072, 3072], P('tp', 'dp')
Inputs may be any that keep to these rules, and one draw needn't show every extreme that they name: `tile_map`: the positions within each row are distinct. `windows`: the time reach is 0 or 1; the first tile of every time slab has time reach 1 and spatial reach 2.
All inputs are finite; a program needn't handle non-finite values.
Results may differ from a plain program's by a relative error of at most 0.024.
Values may be sent and summed in bfloat16 or wider, within the bound.
A program may use at most 64 MiB of HBM per device.

v0:
```python
import jax
import jax.numpy as jnp
from jax import lax
from jax.sharding import PartitionSpec as P

HD = 128
TILE = 384


def in_order(parts, dim):
    shape = list(parts.shape[1:])
    shape[dim] *= parts.shape[0]
    return jnp.moveaxis(parts, 0, dim).reshape(shape)


def from_everyone(shard, axis):
    copies = jnp.broadcast_to(shard, (lax.axis_size(axis), *shard.shape))
    return lax.all_to_all(copies, axis, split_axis=0, concat_axis=0, tiled=True)


def gathered_copies(shard, axis, dim):
    return in_order(from_everyone(shard, axis), dim)


def padded(cells, sides, width):
    for axis, dim in sides:
        count = lax.axis_size(axis)
        ends = count - 1
        head = lax.slice_in_dim(cells, 0, width, axis=dim)
        tail = lax.slice_in_dim(cells, cells.shape[dim] - width, cells.shape[dim], axis=dim)
        cells = jnp.concatenate(
            [
                lax.ppermute(tail, axis, [(i, (i + 1) % count) for i in range(ends)]),
                cells,
                lax.ppermute(head, axis, [((i + 1) % count, i) for i in range(ends)]),
            ],
            axis=dim,
        )
    return cells


def shifted(block, axis, distance):
    devices = range(lax.axis_size(axis))
    route = [(i - distance, i) for i in devices if i - distance in devices]
    return lax.ppermute(block, axis, route)


def cut_along(shard, dim, count):
    shape = shard.shape
    parts = shard.reshape(*shape[:dim], count, shape[dim] // count, *shape[dim + 1 :])
    return jnp.moveaxis(parts, dim, 0)


def summed_on_arrival(shard, axis, dim):
    count = lax.axis_size(axis)
    parts = lax.all_to_all(cut_along(shard, dim, count), axis, 0, 0, tiled=True)
    return jnp.sum(parts.astype(jnp.float32), axis=0)


def window_mask(own_map, side_maps, valid, spans, text_live):
    reach = jnp.abs(jnp.arange(3, dtype=jnp.int32) - 1)
    near_time = reach[None, :, None] <= spans[:, 0][:, None, None]
    near_space = (
        jnp.abs(own_map[:, None, None] - side_maps[None, :, :]) <= spans[:, 1][:, None, None]
    )
    allowed = near_time & near_space & valid[None, :, None]
    count = own_map.shape[0]
    tiles = allowed.reshape(count, 3 * count)
    video = jnp.broadcast_to(tiles[:, None, :, None], (count, TILE, 3 * count, TILE))
    video = video.reshape(count * TILE, 3 * count * TILE)
    text = jnp.broadcast_to(text_live[None, :], (count * TILE, text_live.shape[0]))
    return jnp.concatenate([video, text], axis=1)


def tile_attention(query, keys, values, grad_attn, allowed):
    factor = HD ** (-0.5)
    scores = factor * jnp.dot(query, keys.T, preferred_element_type=jnp.float32)
    scores = jnp.where(allowed, scores, -1e30)
    top = jnp.max(scores, axis=1, keepdims=True)
    weights = jnp.exp(scores - top)
    weights = weights / jnp.sum(weights, axis=1, keepdims=True)
    probs = weights.astype(jnp.bfloat16)
    attended = jnp.dot(probs, values, preferred_element_type=jnp.float32).astype(jnp.bfloat16)
    delta = jnp.sum(
        grad_attn.astype(jnp.float32) * attended.astype(jnp.float32), axis=1, keepdims=True
    )
    grad_probs = jnp.dot(grad_attn, values.T, preferred_element_type=jnp.float32)
    grad_scores = (weights * (grad_probs - delta)).astype(jnp.bfloat16)
    grad_query = factor * jnp.dot(grad_scores, keys, preferred_element_type=jnp.float32)
    grad_keys = factor * jnp.dot(grad_scores.T, query, preferred_element_type=jnp.float32)
    grad_values = jnp.dot(probs.T, grad_attn, preferred_element_type=jnp.float32)
    return (attended, grad_query, grad_keys, grad_values)


def per_device(
    query,
    key,
    value,
    text_key,
    text_value,
    grad_out,
    gate,
    out_weight,
    windows,
    tile_map,
    text_count,
):
    own_query = query[0]
    tok = own_query.shape[0]
    width = own_query.shape[1]
    full_grad = lax.all_gather(grad_out[0], "tp", axis=1, tiled=True)
    scaled = (full_grad.astype(jnp.float32) * gate[0].astype(jnp.float32)[None, :]).astype(
        jnp.bfloat16
    )
    grad_attn = lax.dot_general(
        scaled,
        gathered_copies(out_weight, "dp", 1),
        (((1,), (1,)), ((), ())),
        preferred_element_type=jnp.float32,
    )
    grad_attn = grad_attn.astype(jnp.bfloat16)
    paired = jnp.stack([key[0], value[0]], axis=0)
    extended = padded(paired, (("sp", 1),), tok)
    index = lax.axis_index("sp")
    slabs = lax.axis_size("sp")
    tiles_here = tile_map.shape[1]
    blank = jnp.zeros((1, tiles_here), jnp.int32)
    padded_map = jnp.concatenate([blank, tile_map, blank], axis=0)
    own_map = lax.dynamic_index_in_dim(tile_map, index, 0, keepdims=False)
    side_maps = lax.dynamic_slice_in_dim(padded_map, index, 3, 0)
    others = index + jnp.arange(3, dtype=jnp.int32) - 1
    valid = (others >= 0) & (others < slabs)
    text_live = jnp.arange(text_key.shape[1], dtype=jnp.int32) < text_count[0]
    allowed = window_mask(own_map, side_maps, valid, windows, text_live)
    results = [[], [], [], []]
    for head in range(width // HD):
        lower = head * HD
        upper = lower + HD
        all_k = jnp.concatenate([extended[0][:, lower:upper], text_key[0][:, lower:upper]], axis=0)
        all_v = jnp.concatenate(
            [extended[1][:, lower:upper], text_value[0][:, lower:upper]], axis=0
        )
        outcome = tile_attention(
            own_query[:, lower:upper], all_k, all_v, grad_attn[:, lower:upper], allowed
        )
        for place in range(4):
            results[place].append(outcome[place])
    attended = jnp.concatenate(results[0], axis=1)
    grad_q = jnp.concatenate(results[1], axis=1)
    grad_k = jnp.concatenate(results[2], axis=1)
    grad_v = jnp.concatenate(results[3], axis=1)
    earlier = jnp.stack([grad_k[:tok], grad_v[:tok]], axis=0)
    later = jnp.stack([grad_k[2 * tok : 3 * tok], grad_v[2 * tok : 3 * tok]], axis=0)
    from_later = shifted(earlier.astype(jnp.bfloat16), "sp", -1).astype(earlier.dtype)
    from_earlier = shifted(later.astype(jnp.bfloat16), "sp", 1).astype(later.dtype)
    own_k = grad_k[tok : 2 * tok] + from_later[0] + from_earlier[0]
    own_v = grad_v[tok : 2 * tok] + from_later[1] + from_earlier[1]
    text_k, text_v = (
        lax.psum(grad_k[3 * tok :].astype(jnp.bfloat16), "sp").astype(jnp.float32),
        lax.psum(grad_v[3 * tok :].astype(jnp.bfloat16), "sp").astype(jnp.float32),
    )
    local_weight = lax.dot_general(
        attended, scaled, (((0,), (0,)), ((), ())), preferred_element_type=jnp.float32
    )
    spread = summed_on_arrival(local_weight.astype(jnp.bfloat16), ("dp", "sp"), 1)
    weight_grad = gathered_copies(spread, "sp", 1)
    return (
        grad_q.astype(jnp.bfloat16)[None],
        own_k.astype(jnp.bfloat16)[None],
        own_v.astype(jnp.bfloat16)[None],
        text_k.astype(jnp.bfloat16)[None],
        text_v.astype(jnp.bfloat16)[None],
        weight_grad,
    )


def solution(mesh):
    placed = (
        P("dp", "sp", "tp"),
        P("dp", "sp", "tp"),
        P("dp", "sp", "tp"),
        P("dp", None, "tp"),
        P("dp", None, "tp"),
        P("dp", "sp", "tp"),
        P("dp", None),
        P("tp", "dp"),
        P("sp", None),
        P(),
        P("dp"),
    )
    return jax.shard_map(
        per_device,
        mesh=mesh,
        in_specs=placed,
        out_specs=(
            P("dp", "sp", "tp"),
            P("dp", "sp", "tp"),
            P("dp", "sp", "tp"),
            P("dp", None, "tp"),
            P("dp", None, "tp"),
            P("tp", "dp"),
        ),
        check_vma=False,
    )
```

profile of v0, /device:TPU:32, one launch (start us, length us, event | category | flops | bytes accessed | tf_op | source)
XLA Modules:
  0.0 227.6 jit_solution(2305887054889296009)
XLA Ops:
  10.5 4.6 %collective-permute-start = (bf16[2,384,384]{2,1,0:T(8,128)(2,1)S(1)}, bf16[2,384,384]{2,1,0:T(8,128)(2,1)S(1)}, u32[]{:S(2)}, u32[]{:S(2)}) collective-permute-start(bf16[2,384,384]{2,1,0:T(8,128)(2,1)S(1)} %constant_dynamic-update-slice_fusion), channel_id=1, source_target_pairs={{0,8},{8,16},{16,24},{24,32},{32,40},{40,48},{48,56},{1,9},{9,17},... | collective-permute-start | bytes 1769480 | tf_op jit(solution)/shard_map/ppermute | solution.py:33
  16.4 1.7 broadcast_in_dim.59
  18.1 4.6 %all-to-all-start = ((bf16[4,384,768]{1,2,0:T(8,128)(2,1)}), bf16[4,384,768]{1,2,0:T(8,128)(2,1)}, u32[]{:S(2)}, u32[]{:S(2)}) async-start(bf16[4,384,768]{1,2,0:T(8,128)(2,1)} %broadcast_in_dim.59), calls=%async_computation | async-start | bytes 4718592 | tf_op jit(solution)/shard_map/all_to_all | solution.py:18
  25.4 2.0 fusion.62
  37.3 23.3 %all-to-all-done = bf16[4,384,768]{1,2,0:T(8,128)(2,1)} async-done(((bf16[4,384,768]{1,2,0:T(8,128)(2,1)}), bf16[4,384,768]{1,2,0:T(8,128)(2,1)}, u32[]{:S(2)}, u32[]{:S(2)}) %all-to-all-start) | async-done | bytes 2359328 | tf_op jit(solution)/shard_map/all_to_all | solution.py:18
  60.5 11.3 %all-gather.3.cloned.1.call-done = bf16[1,384,3072]{2,1,0:T(8,128)(2,1)} async-done(((bf16[1,384,384]{2,1,0:T(8,128)(2,1)}), bf16[1,384,3072]{2,1,0:T(8,128)(2,1)}) %all-gather.3.cloned.1.call-update) | async-done | bytes 2359312 | tf_op jit(solution)/shard_map/all_gather | solution.py:111
  71.8 4.0 %fusion.22 = bf16[384,384]{0,1:T(8,128)(2,1)S(1)} fusion(bf16[384,3072]{0,1:T(8,128)(2,1)} %bitcast.12, bf16[1,384,3072]{2,1,0:T(8,128)(2,1)} %all-gather.3.cloned.1.call-done, f32[3072]{0:T(1024)S(1)} %bitcast.122), kind=kOutput, calls=%fused_computation.38 | convolution fusion | flops 909656064 | bytes 5025792 | tf_op jit(solution)/shard_map/dot_general | solution.py:115
  80.4 1.6 fusion.11
  82.3 1.6 fusion.12
  83.9 2.2 convolution_multiply_fusion.3
  87.5 2.5 %copy.29 = bf16[384,3072]{0,1:T(8,128)(2,1)} copy(bf16[384,3072]{1,0:T(8,128)(2,1)S(1)} %convolution_convert_fusion) | data formatting | bytes 4718592 | tf_op jit(solution)/shard_map/convert_element_type | solution.py:165
  90.0 7.3 %all-to-all-start.1 = ((bf16[32,384,96]{1,2,0:T(8,128)(2,1)}), bf16[32,384,96]{1,2,0:T(8,128)(2,1)S(1)}, u32[]{:S(2)}, u32[]{:S(2)}) async-start(bf16[32,384,96]{1,2,0:T(8,128)(2,1)} %bitcast.112), calls=%async_computation.1 | async-start | bytes 4718592 | tf_op jit(solution)/shard_map/all_to_all | solution.py:56
  97.3 1.5 fusion.76
  102.5 4.5 %collective-permute-start.3 = (bf16[2,384,384]{1,2,0:T(8,128)(2,1)}, bf16[2,384,384]{1,2,0:T(8,128)(2,1)}, u32[]{:S(2)}, u32[]{:S(2)}) collective-permute-start(bf16[2,384,384]{1,2,0:T(8,128)(2,1)} %pad_maximum_fusion.4), channel_id=1, source_target_pairs={{0,8},{8,16},{16,24},{24,32},{32,40},{40,48},{48,56},{1,9},{9,17},... | collective-permute-start | bytes 1769480 | tf_op jit(solution)/shard_map/ppermute | solution.py:45
  110.6 1.8 fusion.28
  112.4 1.5 pad_maximum_fusion.1
  113.9 14.7 %all-to-all-done.1 = bf16[32,384,96]{1,2,0:T(8,128)(2,1)S(1)} async-done(((bf16[32,384,96]{1,2,0:T(8,128)(2,1)}), bf16[32,384,96]{1,2,0:T(8,128)(2,1)S(1)}, u32[]{:S(2)}, u32[]{:S(2)}) %all-to-all-start.1) | async-done | bytes 2359328 | tf_op jit(solution)/shard_map/all_to_all | solution.py:56
  130.1 6.7 %all-to-all-start.2 = ((f32[8,384,96]{1,2,0:T(8,128)}), f32[8,384,96]{1,2,0:T(8,128)S(1)}, u32[]{:S(2)}, u32[]{:S(2)}) async-start(f32[8,384,96]{1,2,0:T(8,128)} %broadcast_in_dim.64), calls=%async_computation.2 | async-start | bytes 2359296 | tf_op jit(solution)/shard_map/all_to_all | solution.py:18
  136.8 1.9 fusion.29
  138.7 1.7 fusion.30
  141.1 1.8 copy.30
  144.5 65.8 %all-reduce.3.cloned.1.call-done = (bf16[1,256,384]{1,2,0:T(8,128)(2,1)}, bf16[1,256,384]{1,2,0:T(8,128)(2,1)}) async-done(((bf16[1,256,384]{1,2,0:T(8,128)(2,1)}, bf16[1,256,384]{1,2,0:T(8,128)(2,1)}), (bf16[1,256,384]{1,2,0:T(8,128)(2,1)}, bf16[1,256,384]{1,2,0:T(8,128)(2,1)})) %all-reduce.3.cloned.1.call-update) | async-done | bytes 393232 | tf_op jit(solution)/shard_map/psum | solution.py:159
  210.3 1.7 copy.33
  212.0 1.7 copy.34
  (145 shorter events, 40.3 us)
Async XLA Ops:
  9.2 18.5 %collective-permute-start.1 = (bf16[2,384,384]{2,1,0:T(8,128)(2,1)S(1)}, bf16[2,384,384]{2,1,0:T(8,128)(2,1)S(1)}, u32[]{:S(2)}, u32[]{:S(2)}) collective-permute-start(bf16[2,384,384]{2,1,0:T(8,128)(2,1)S(1)} %constant_dynamic-update-slice_fusion), channel_id=1, source_target_pairs={{8,0},{16,8},{24,16},{32,24},{40,32},{48,40},{56,48},{9,1},{17,9},... | collective-permute-start | bytes 1769480 | tf_op jit(solution)/shard_map/ppermute | solution.py:35
  10.5 17.2 %collective-permute-start = (bf16[2,384,384]{2,1,0:T(8,128)(2,1)S(1)}, bf16[2,384,384]{2,1,0:T(8,128)(2,1)S(1)}, u32[]{:S(2)}, u32[]{:S(2)}) collective-permute-start(bf16[2,384,384]{2,1,0:T(8,128)(2,1)S(1)} %constant_dynamic-update-slice_fusion), channel_id=1, source_target_pairs={{0,8},{8,16},{16,24},{24,32},{32,40},{40,48},{48,56},{1,9},{9,17},... | collective-permute-start | bytes 1769480 | tf_op jit(solution)/shard_map/ppermute | solution.py:33
  18.1 6.1 %copy-start.36 = (s32[1,2]{1,0:T(1,128)S(1)}, s32[1,2]{1,0:T(1,128)}, u32[]{:S(2)}) copy-start(s32[1,2]{1,0:T(1,128)} %param.19) | copy-start | bytes 28
  18.1 6.7 %copy-start.38 = (s32[8,1]{0,1:T(1,128)S(1)}, s32[8,1]{0,1:T(1,128)}, u32[]{:S(2)}) copy-start(s32[8,1]{0,1:T(1,128)} %param.20) | copy-start | bytes 100
  18.1 9.3 %copy-start.35 = (bf16[1,3072]{1,0:T(2,128)(2,1)S(1)}, bf16[1,3072]{1,0:T(2,128)(2,1)}, u32[]{:S(2)}) copy-start(bf16[1,3072]{1,0:T(2,128)(2,1)} %param.17) | copy-start | bytes 18436
  18.1 9.5 %copy-start.29 = (bf16[1,256,384]{2,1,0:T(8,128)(2,1)S(1)}, bf16[1,256,384]{2,1,0:T(8,128)(2,1)}, u32[]{:S(2)}) copy-start(bf16[1,256,384]{2,1,0:T(8,128)(2,1)} %param.14) | copy-start | bytes 589828
  18.1 9.5 %copy-start.30 = (bf16[1,256,384]{2,1,0:T(8,128)(2,1)S(1)}, bf16[1,256,384]{2,1,0:T(8,128)(2,1)}, u32[]{:S(2)}) copy-start(bf16[1,256,384]{2,1,0:T(8,128)(2,1)} %param.15) | copy-start | bytes 589828
  18.1 42.4 %all-to-all-start = ((bf16[4,384,768]{1,2,0:T(8,128)(2,1)}), bf16[4,384,768]{1,2,0:T(8,128)(2,1)}, u32[]{:S(2)}, u32[]{:S(2)}) async-start(bf16[4,384,768]{1,2,0:T(8,128)(2,1)} %broadcast_in_dim.59), calls=%async_computation | async-start | bytes 4718592 | tf_op jit(solution)/shard_map/all_to_all | solution.py:18
  22.8 49.1 %all-gather.3.cloned.1.call-start = ((), (), s32[]{:S(2)}) async-start(), calls=%async_computation.3 | async-start | bytes 2654208 | tf_op jit(solution)/shard_map/all_gather | solution.py:111
  27.7 6.2 %copy-start.33 = (bf16[256,128]{1,0:T(8,128)(2,1)}, bf16[256,128]{1,0:T(8,128)(2,1)S(1)}, u32[]{:S(2)}) copy-start(bf16[256,128]{1,0:T(8,128)(2,1)S(1)} %get-tuple-element.37) | copy-start | bytes 196612
  29.1 4.7 %copy-start.25 = (bf16[1152,128]{1,0:T(8,128)(2,1)}, bf16[1152,128]{1,0:T(8,128)(2,1)S(1)}, u32[]{:S(2)}) copy-start(bf16[1152,128]{1,0:T(8,128)(2,1)S(1)} %get-tuple-element.31) | copy-start | bytes 884740
  31.6 4.3 %copy-start = (f32[384,1408]{0,1:T(8,128)}, f32[384,1408]{0,1:T(8,128)S(1)}, u32[]{:S(2)}) copy-start(f32[384,1408]{0,1:T(8,128)S(1)} %get-tuple-element.46) | copy-start | bytes 6488068
  71.8 4.0 %copy-start.16 = (bf16[384,1408]{0,1:T(8,128)(2,1)S(1)}, bf16[384,1408]{0,1:T(8,128)(2,1)}, u32[]{:S(2)}) copy-start(bf16[384,1408]{0,1:T(8,128)(2,1)} %copy-done.15) | copy-start | bytes 3244036
  71.8 4.4 %copy-start.14 = (bf16[384,1408]{0,1:T(8,128)(2,1)S(1)}, bf16[384,1408]{0,1:T(8,128)(2,1)}, u32[]{:S(2)}) copy-start(bf16[384,1408]{0,1:T(8,128)(2,1)} %copy-done.13) | copy-start | bytes 3244036
  80.1 3.8 %copy-start.19 = (bf16[384,1408]{0,1:T(8,128)(2,1)}, bf16[384,1408]{0,1:T(8,128)(2,1)S(1)}, u32[]{:S(2)}) copy-start(bf16[384,1408]{0,1:T(8,128)(2,1)S(1)} %fusion.10) | copy-start | bytes 3244036
  82.3 3.8 %copy-start.37 = (bf16[1,384,3072]{2,1,0:T(8,128)(2,1)S(1)}, bf16[1,384,3072]{2,1,0:T(8,128)(2,1)}, u32[]{:S(2)}) copy-start(bf16[1,384,3072]{2,1,0:T(8,128)(2,1)} %all-gather.3.cloned.1.call-done) | copy-start | bytes 7077892
  90.0 38.7 %all-to-all-start.1 = ((bf16[32,384,96]{1,2,0:T(8,128)(2,1)}), bf16[32,384,96]{1,2,0:T(8,128)(2,1)S(1)}, u32[]{:S(2)}, u32[]{:S(2)}) async-start(bf16[32,384,96]{1,2,0:T(8,128)(2,1)} %bitcast.112), calls=%async_computation.1 | async-start | bytes 4718592 | tf_op jit(solution)/shard_map/all_to_all | solution.py:56
  97.3 113.0 %all-reduce.3.cloned.1.call-start = ((), (), s32[]{:S(2)}) async-start(), calls=%async_computation.4 | async-start | bytes 786432 | tf_op jit(solution)/shard_map/psum | solution.py:159
  102.5 111.3 %collective-permute-start.3 = (bf16[2,384,384]{1,2,0:T(8,128)(2,1)}, bf16[2,384,384]{1,2,0:T(8,128)(2,1)}, u32[]{:S(2)}, u32[]{:S(2)}) collective-permute-start(bf16[2,384,384]{1,2,0:T(8,128)(2,1)} %pad_maximum_fusion.4), channel_id=1, source_target_pairs={{0,8},{8,16},{16,24},{24,32},{32,40},{40,48},{48,56},{1,9},{9,17},... | collective-permute-start | bytes 1769480 | tf_op jit(solution)/shard_map/ppermute | solution.py:45
  107.9 107.0 %collective-permute-start.2 = (bf16[2,384,384]{1,2,0:T(8,128)(2,1)}, bf16[2,384,384]{1,2,0:T(8,128)(2,1)}, u32[]{:S(2)}, u32[]{:S(2)}) collective-permute-start(bf16[2,384,384]{1,2,0:T(8,128)(2,1)} %pad_maximum_fusion.3), channel_id=1, source_target_pairs={{8,0},{16,8},{24,16},{32,24},{40,32},{48,40},{56,48},{9,1},{17,9},... | collective-permute-start | bytes 1769480 | tf_op jit(solution)/shard_map/ppermute | solution.py:45
  130.1 89.3 %all-to-all-start.2 = ((f32[8,384,96]{1,2,0:T(8,128)}), f32[8,384,96]{1,2,0:T(8,128)S(1)}, u32[]{:S(2)}, u32[]{:S(2)}) async-start(f32[8,384,96]{1,2,0:T(8,128)} %broadcast_in_dim.64), calls=%async_computation.2 | async-start | bytes 2359296 | tf_op jit(solution)/shard_map/all_to_all | solution.py:18
  136.8 6.2 %copy-start.7 = (f32[1408,128]{0,1:T(8,128)S(1)}, f32[1408,128]{0,1:T(8,128)}, u32[]{:S(2)}) copy-start(f32[1408,128]{0,1:T(8,128)} %convolution_multiply_fusion.3) | copy-start | bytes 2162692
  136.8 6.2 %copy-start.9 = (f32[1408,128]{0,1:T(8,128)S(1)}, f32[1408,128]{0,1:T(8,128)}, u32[]{:S(2)}) copy-start(f32[1408,128]{0,1:T(8,128)} %copy-done.8) | copy-start | bytes 2162692
  136.8 6.2 %copy-start.11 = (f32[1408,128]{0,1:T(8,128)S(1)}, f32[1408,128]{0,1:T(8,128)}, u32[]{:S(2)}) copy-start(f32[1408,128]{0,1:T(8,128)} %copy-done.10) | copy-start | bytes 2162692
  (26 other events, 46.7 us)
Sparse Core Ops, SparseCore 0:
  25.4 46.3 all-gather.2
  110.7 99.5 all-reduce.2
where the time goes:
time: 229 us; the launch traced here: 228 us
  waiting for transfers between devices  116 us (51%)
  starting transfers between devices  30.3 us (13%)
  matrix products  24.9 us (11%)
  local copies, waits for them, and re-layouts  24.4 us (11%)
  other arithmetic  16.9 us (7%)
  between operations  15.2 us (7%)
    psum x1, waiting for transfers between devices, per_device(): lax.psum(grad_k[3 * tok:].astype(jnp.bfloat16), 'sp').astype(jnp.float32)  65.8 us
    all_to_all x2, waiting for transfers between devices, from_everyone(): return lax.all_to_all(copies, axis, split_axis=0, concat_axis=0, tiled=True)  23.3 us
    all_to_all x1, waiting for transfers between devices, summed_on_arrival(): parts = lax.all_to_all(cut_along(shard, dim, count), axis, 0, 0, tiled=True)  14.7 us
    unnamed x90, local copies, waits for them, and re-layouts  14.2 us
    all_to_all x2, starting transfers between devices, from_everyone(): return lax.all_to_all(copies, axis, split_axis=0, concat_axis=0, tiled=True)  11.3 us
    all_gather x1, waiting for transfers between devices, per_device(): full_grad = lax.all_gather(grad_out[0], 'tp', axis=1, tiled=True)  11.3 us
    all_to_all x1, starting transfers between devices, summed_on_arrival(): parts = lax.all_to_all(cut_along(shard, dim, count), axis, 0, 0, tiled=True)  7.3 us
    ppermute x2, starting transfers between devices, shifted(): return lax.ppermute(block, axis, route)  5.78 us
  transfers between devices with their start and end apart: 9, of which 4 were waited for; matrix products, arithmetic and copies ran while one was open for 19% of the time, Pallas kernels for 0%

commit v1 on v0

--- a/solution.py
+++ b/solution.py
@@ -108,7 +108,9 @@
     own_query = query[0]
     tok = own_query.shape[0]
     width = own_query.shape[1]
-    full_grad = lax.all_gather(grad_out[0], "tp", axis=1, tiled=True)
+    full_grad = jnp.concatenate(
+        lax.all_to_all(jnp.stack([grad_out[0]] * lax.axis_size("tp")), "tp", 0, 0), axis=1
+    )
     scaled = (full_grad.astype(jnp.float32) * gate[0].astype(jnp.float32)[None, :]).astype(
         jnp.bfloat16
     )

time: 229 us -> 298 us (1.30)
  waiting for transfers between devices: 116 us -> 155 us
  local copies, waits for them, and re-layouts: 24.4 us -> 37.1 us
  starting transfers between devices: 30.3 us -> 40 us
  other arithmetic: 16.9 us -> 24.5 us
    all_to_all x0 -> x1, waiting for transfers between devices: none -> 32.8 us  [per_device(): lax.all_to_all(jnp.stack([grad_out[0]] * lax.axis_size('tp')), 'tp', 0, 0)]
    psum x1, waiting for transfers between devices: 65.8 us -> 85.8 us  [per_device(): lax.psum(grad_k[3 * tok:].astype(jnp.bfloat16), 'sp').astype(jnp.float32)]
    all_gather x1 -> x0, waiting for transfers between devices: 11.3 us -> none  [per_device(): full_grad = lax.all_gather(grad_out[0], 'tp', axis=1, tiled=True)]
    all_to_all x0 -> x1, starting transfers between devices: none -> 8.7 us  [per_device(): lax.all_to_all(jnp.stack([grad_out[0]] * lax.axis_size('tp')), 'tp', 0, 0)]
    unnamed x90 -> x108, local copies, waits for them, and re-layouts: 14.2 us -> 19.6 us
where the time goes in v1:
time: 298 us; the launch traced here: 297 us
  waiting for transfers between devices  155 us (52%)
  starting transfers between devices  40 us (13%)
  local copies, waits for them, and re-layouts  37.1 us (12%)
  matrix products  24.6 us (8%)
  other arithmetic  24.5 us (8%)
  between operations  15.3 us (5%)
    psum x1, waiting for transfers between devices, per_device(): lax.psum(grad_k[3 * tok:].astype(jnp.bfloat16), 'sp').astype(jnp.float32)  85.8 us
    all_to_all x1, waiting for transfers between devices, per_device(): lax.all_to_all(jnp.stack([grad_out[0]] * lax.axis_size('tp')), 'tp', 0, 0)  32.8 us
    all_to_all x2, waiting for transfers between devices, from_everyone(): return lax.all_to_all(copies, axis, split_axis=0, concat_axis=0, tiled=True)  20.9 us
    unnamed x108, local copies, waits for them, and re-layouts  19.6 us
    all_to_all x1, waiting for transfers between devices, summed_on_arrival(): parts = lax.all_to_all(cut_along(shard, dim, count), axis, 0, 0, tiled=True)  15.7 us
    all_to_all x2, starting transfers between devices, from_everyone(): return lax.all_to_all(copies, axis, split_axis=0, concat_axis=0, tiled=True)  11.5 us
    all_to_all x1, starting transfers between devices, per_device(): lax.all_to_all(jnp.stack([grad_out[0]] * lax.axis_size('tp')), 'tp', 0, 0)  8.7 us
    all_to_all x1, starting transfers between devices, summed_on_arrival(): parts = lax.all_to_all(cut_along(shard, dim, count), axis, 0, 0, tiled=True)  7.29 us
  transfers between devices with their start and end apart: 9, of which 4 were waited for; matrix products, arithmetic and copies ran while one was open for 19% of the time, Pallas kernels for 0%

profile of v1, /device:TPU:32, one launch (start us, length us, event | category | flops | bytes accessed | tf_op | source)
XLA Modules:
  0.0 296.6 jit_solution(4811717579091327066)
XLA Ops:
  10.5 5.4 %collective-permute-start = (bf16[2,384,384]{2,1,0:T(8,128)(2,1)S(1)}, bf16[2,384,384]{2,1,0:T(8,128)(2,1)}, u32[]{:S(2)}, u32[]{:S(2)}) collective-permute-start(bf16[2,384,384]{2,1,0:T(8,128)(2,1)S(1)} %constant_dynamic-update-slice_fusion), channel_id=1, source_target_pairs={{0,8},{8,16},{16,24},{24,32},{32,40},{40,48},{48,56},{1,9},{9,17},... | collective-permute-start | bytes 1769480 | tf_op jit(solution)/shard_map/ppermute | solution.py:33
  17.0 1.7 stack.31
  18.7 8.7 %all-to-all-start = ((bf16[8,384,384]{1,2,0:T(8,128)(2,1)}), bf16[8,384,384]{1,2,0:T(8,128)(2,1)S(1)}, u32[]{:S(2)}, u32[]{:S(2)}) async-start(bf16[8,384,384]{1,2,0:T(8,128)(2,1)} %stack.31), calls=%async_computation | async-start | bytes 4718592 | tf_op jit(solution)/shard_map/all_to_all | solution.py:112
  29.8 2.0 fusion.56
  49.4 32.8 %all-to-all-done = bf16[8,384,384]{1,2,0:T(8,128)(2,1)S(1)} async-done(((bf16[8,384,384]{1,2,0:T(8,128)(2,1)}), bf16[8,384,384]{1,2,0:T(8,128)(2,1)S(1)}, u32[]{:S(2)}, u32[]{:S(2)}) %all-to-all-start) | async-done | bytes 2359328 | tf_op jit(solution)/shard_map/all_to_all | solution.py:112
  82.2 1.6 broadcast_in_dim.59
  83.8 4.7 %all-to-all-start.1 = ((bf16[4,384,768]{1,2,0:T(8,128)(2,1)}), bf16[4,384,768]{1,2,0:T(8,128)(2,1)}, u32[]{:S(2)}, u32[]{:S(2)}) async-start(bf16[4,384,768]{1,2,0:T(8,128)(2,1)} %broadcast_in_dim.59), calls=%async_computation.1 | async-start | bytes 4718592 | tf_op jit(solution)/shard_map/all_to_all | solution.py:18
  88.5 2.1 fusion.25
  94.1 1.9 multiply_convert_fusion
  96.0 20.9 %all-to-all-done.1 = bf16[4,384,768]{1,2,0:T(8,128)(2,1)} async-done(((bf16[4,384,768]{1,2,0:T(8,128)(2,1)}), bf16[4,384,768]{1,2,0:T(8,128)(2,1)}, u32[]{:S(2)}, u32[]{:S(2)}) %all-to-all-start.1) | async-done | bytes 2359328 | tf_op jit(solution)/shard_map/all_to_all | solution.py:18
  116.9 3.9 %convolution_convert_fusion.1 = bf16[384,384]{0,1:T(8,128)(2,1)S(1)} fusion(bf16[384,3072]{0,1:T(8,128)(2,1)} %bitcast.118, bf16[384,3072]{0,1:T(8,128)(2,1)} %bitcast.13), kind=kOutput, calls=%fused_computation.38 | convolution fusion | flops 906117120 | bytes 5013504 | tf_op jit(solution)/shard_map/dot_general | solution.py:117
  128.8 2.2 convolution_multiply_fusion.3
  132.9 2.5 copy.30
  135.4 7.3 %all-to-all-start.2 = ((bf16[32,384,96]{1,2,0:T(8,128)(2,1)}), bf16[32,384,96]{1,2,0:T(8,128)(2,1)S(1)}, u32[]{:S(2)}, u32[]{:S(2)}) async-start(bf16[32,384,96]{1,2,0:T(8,128)(2,1)} %bitcast.117), calls=%async_computation.2 | async-start | bytes 4718592 | tf_op jit(solution)/shard_map/all_to_all | solution.py:56
  151.8 4.6 %collective-permute-start.3 = (bf16[2,384,384]{1,2,0:T(8,128)(2,1)}, bf16[2,384,384]{1,2,0:T(8,128)(2,1)}, u32[]{:S(2)}, u32[]{:S(2)}) collective-permute-start(bf16[2,384,384]{1,2,0:T(8,128)(2,1)} %pad_maximum_fusion.4), channel_id=1, source_target_pairs={{0,8},{8,16},{16,24},{24,32},{32,40},{40,48},{48,56},{1,9},{9,17},... | collective-permute-start | bytes 1769480 | tf_op jit(solution)/shard_map/ppermute | solution.py:45
  158.7 15.7 %all-to-all-done.2 = bf16[32,384,96]{1,2,0:T(8,128)(2,1)S(1)} async-done(((bf16[32,384,96]{1,2,0:T(8,128)(2,1)}), bf16[32,384,96]{1,2,0:T(8,128)(2,1)S(1)}, u32[]{:S(2)}, u32[]{:S(2)}) %all-to-all-start.2) | async-done | bytes 2359328 | tf_op jit(solution)/shard_map/all_to_all | solution.py:56
  175.8 6.8 %all-to-all-start.3 = ((f32[8,384,96]{1,2,0:T(8,128)}), f32[8,384,96]{1,2,0:T(8,128)}, u32[]{:S(2)}, u32[]{:S(2)}) async-start(f32[8,384,96]{1,2,0:T(8,128)} %broadcast_in_dim.64), calls=%async_computation.3 | async-start | bytes 2359296 | tf_op jit(solution)/shard_map/all_to_all | solution.py:18
  182.6 2.0 pad_maximum_fusion.3
  185.9 1.7 fusion.24
  188.6 3.6 %pad_maximum_fusion = (f32[1408,384]{0,1:T(8,128)}, f32[1408,384]{0,1:T(8,128)}) fusion(f32[1408,128]{0,1:T(8,128)S(1)} %copy-done.10, f32[1408,128]{0,1:T(8,128)} %copy-done.11, f32[1408,128]{0,1:T(8,128)} %copy-done.12, f32[1408,128]{0,1:T(8,128)S(1)} %fusion.47, f32[1408,128]{0,1:T(8,128)S(1)} %copy-done.7, f32[1408,128]{0,1:T(8,128)S(1)} %copy-done.8), kind=kLoop, calls=%fused_computation.26 | loop fusion | flops 2162688 | bytes 8650752 | tf_op jit(solution)/shard_map/concatenate | solution.py:152
  192.3 85.8 %all-reduce.3.cloned.1.call-done = (bf16[1,256,384]{1,2,0:T(8,128)(2,1)}, bf16[1,256,384]{1,2,0:T(8,128)(2,1)}) async-done(((bf16[1,256,384]{1,2,0:T(8,128)(2,1)}, bf16[1,256,384]{1,2,0:T(8,128)(2,1)}), (bf16[1,256,384]{1,2,0:T(8,128)(2,1)}, bf16[1,256,384]{1,2,0:T(8,128)(2,1)})) %all-reduce.3.cloned.1.call-update) | async-done | bytes 393232 | tf_op jit(solution)/shard_map/psum | solution.py:161
  278.0 1.7 copy.34
  279.7 1.7 copy.35
  287.1 2.7 copy.36
  (166 shorter events, 57.5 us)
Async XLA Ops:
  9.2 29.2 %collective-permute-start.1 = (bf16[2,384,384]{2,1,0:T(8,128)(2,1)S(1)}, bf16[2,384,384]{2,1,0:T(8,128)(2,1)}, u32[]{:S(2)}, u32[]{:S(2)}) collective-permute-start(bf16[2,384,384]{2,1,0:T(8,128)(2,1)S(1)} %constant_dynamic-update-slice_fusion), channel_id=1, source_target_pairs={{8,0},{16,8},{24,16},{32,24},{40,32},{48,40},{56,48},{9,1},{17,9},... | collective-permute-start | bytes 1769480 | tf_op jit(solution)/shard_map/ppermute | solution.py:35
  10.5 27.9 %collective-permute-start = (bf16[2,384,384]{2,1,0:T(8,128)(2,1)S(1)}, bf16[2,384,384]{2,1,0:T(8,128)(2,1)}, u32[]{:S(2)}, u32[]{:S(2)}) collective-permute-start(bf16[2,384,384]{2,1,0:T(8,128)(2,1)S(1)} %constant_dynamic-update-slice_fusion), channel_id=1, source_target_pairs={{0,8},{8,16},{16,24},{24,32},{32,40},{40,48},{48,56},{1,9},{9,17},... | collective-permute-start | bytes 1769480 | tf_op jit(solution)/shard_map/ppermute | solution.py:33
  18.7 8.7 %copy-start.44 = (bf16[1,3072]{1,0:T(2,128)(2,1)S(1)}, bf16[1,3072]{1,0:T(2,128)(2,1)}, u32[]{:S(2)}) copy-start(bf16[1,3072]{1,0:T(2,128)(2,1)} %param.17) | copy-start | bytes 18436
  18.7 9.9 %copy-start.46 = (s32[1,2]{1,0:T(1,128)S(1)}, s32[1,2]{1,0:T(1,128)}, u32[]{:S(2)}) copy-start(s32[1,2]{1,0:T(1,128)} %param.19) | copy-start | bytes 28
  18.7 10.5 %copy-start.47 = (s32[8,1]{0,1:T(1,128)S(1)}, s32[8,1]{0,1:T(1,128)}, u32[]{:S(2)}) copy-start(s32[8,1]{0,1:T(1,128)} %param.20) | copy-start | bytes 100
  18.7 63.5 %all-to-all-start = ((bf16[8,384,384]{1,2,0:T(8,128)(2,1)}), bf16[8,384,384]{1,2,0:T(8,128)(2,1)S(1)}, u32[]{:S(2)}, u32[]{:S(2)}) async-start(bf16[8,384,384]{1,2,0:T(8,128)(2,1)} %stack.31), calls=%async_computation | async-start | bytes 4718592 | tf_op jit(solution)/shard_map/all_to_all | solution.py:112
  36.8 7.0 %copy-start.34 = (bf16[256,128]{1,0:T(8,128)(2,1)}, bf16[256,128]{1,0:T(8,128)(2,1)S(1)}, u32[]{:S(2)}) copy-start(bf16[256,128]{1,0:T(8,128)(2,1)S(1)} %get-tuple-element.42) | copy-start | bytes 196612
  38.4 9.0 %copy-start.41 = (bf16[256,128]{1,0:T(8,128)(2,1)}, bf16[256,128]{1,0:T(8,128)(2,1)S(1)}, u32[]{:S(2)}) copy-start(bf16[256,128]{1,0:T(8,128)(2,1)S(1)} %get-tuple-element.38) | copy-start | bytes 196612
  41.4 5.6 %copy-start.3 = (f32[384,1408]{0,1:T(8,128)}, f32[384,1408]{0,1:T(8,128)S(1)}, u32[]{:S(2)}) copy-start(f32[384,1408]{0,1:T(8,128)S(1)} %get-tuple-element.48) | copy-start | bytes 6488068
  83.8 33.0 %all-to-all-start.1 = ((bf16[4,384,768]{1,2,0:T(8,128)(2,1)}), bf16[4,384,768]{1,2,0:T(8,128)(2,1)}, u32[]{:S(2)}, u32[]{:S(2)}) async-start(bf16[4,384,768]{1,2,0:T(8,128)(2,1)} %broadcast_in_dim.59), calls=%async_computation.1 | async-start | bytes 4718592 | tf_op jit(solution)/shard_map/all_to_all | solution.py:18
  135.4 38.9 %all-to-all-start.2 = ((bf16[32,384,96]{1,2,0:T(8,128)(2,1)}), bf16[32,384,96]{1,2,0:T(8,128)(2,1)S(1)}, u32[]{:S(2)}, u32[]{:S(2)}) async-start(bf16[32,384,96]{1,2,0:T(8,128)(2,1)} %bitcast.117), calls=%async_computation.2 | async-start | bytes 4718592 | tf_op jit(solution)/shard_map/all_to_all | solution.py:56
  150.0 6.4 %copy-start.20 = (bf16[384,1408]{0,1:T(8,128)(2,1)S(1)}, bf16[384,1408]{0,1:T(8,128)(2,1)}, u32[]{:S(2)}) copy-start(bf16[384,1408]{0,1:T(8,128)(2,1)} %copy-done.19) | copy-start | bytes 3244036
  150.0 6.4 %copy-start.26 = (bf16[1152,128]{1,0:T(8,128)(2,1)S(1)}, bf16[1152,128]{1,0:T(8,128)(2,1)}, u32[]{:S(2)}) copy-start(bf16[1152,128]{1,0:T(8,128)(2,1)} %copy-done.25) | copy-start | bytes 884740
  150.0 6.4 %copy-start.39 = (bf16[256,128]{1,0:T(8,128)(2,1)S(1)}, bf16[256,128]{1,0:T(8,128)(2,1)}, u32[]{:S(2)}) copy-start(bf16[256,128]{1,0:T(8,128)(2,1)} %copy-done.38) | copy-start | bytes 196612
  150.0 6.8 %copy-start.24 = (bf16[1152,128]{1,0:T(8,128)(2,1)S(1)}, bf16[1152,128]{1,0:T(8,128)(2,1)}, u32[]{:S(2)}) copy-start(bf16[1152,128]{1,0:T(8,128)(2,1)} %copy-done.23) | copy-start | bytes 884740
  150.0 6.8 %copy-start.37 = (bf16[256,128]{1,0:T(8,128)(2,1)S(1)}, bf16[256,128]{1,0:T(8,128)(2,1)}, u32[]{:S(2)}) copy-start(bf16[256,128]{1,0:T(8,128)(2,1)} %copy-done.36) | copy-start | bytes 196612
  151.8 129.7 %collective-permute-start.3 = (bf16[2,384,384]{1,2,0:T(8,128)(2,1)}, bf16[2,384,384]{1,2,0:T(8,128)(2,1)}, u32[]{:S(2)}, u32[]{:S(2)}) collective-permute-start(bf16[2,384,384]{1,2,0:T(8,128)(2,1)} %pad_maximum_fusion.4), channel_id=1, source_target_pairs={{0,8},{8,16},{16,24},{24,32},{32,40},{40,48},{48,56},{1,9},{9,17},... | collective-permute-start | bytes 1769480 | tf_op jit(solution)/shard_map/ppermute | solution.py:45
  174.7 11.3 %copy-start.35 = (bf16[256,128]{1,0:T(8,128)(2,1)S(1)}, bf16[256,128]{1,0:T(8,128)(2,1)}, u32[]{:S(2)}) copy-start(bf16[256,128]{1,0:T(8,128)(2,1)} %copy-done.34) | copy-start | bytes 196612
  175.8 111.3 %all-to-all-start.3 = ((f32[8,384,96]{1,2,0:T(8,128)}), f32[8,384,96]{1,2,0:T(8,128)}, u32[]{:S(2)}, u32[]{:S(2)}) async-start(f32[8,384,96]{1,2,0:T(8,128)} %broadcast_in_dim.64), calls=%async_computation.3 | async-start | bytes 2359296 | tf_op jit(solution)/shard_map/all_to_all | solution.py:18
  182.6 95.4 %all-reduce.3.cloned.1.call-start = ((), (), s32[]{:S(2)}) async-start(), calls=%async_computation.4 | async-start | bytes 786432 | tf_op jit(solution)/shard_map/psum | solution.py:161
  182.6 6.0 %copy-start.7 = (f32[1408,128]{0,1:T(8,128)S(1)}, f32[1408,128]{0,1:T(8,128)}, u32[]{:S(2)}) copy-start(f32[1408,128]{0,1:T(8,128)} %fusion.50) | copy-start | bytes 2162692
  182.6 6.0 %copy-start.8 = (f32[1408,128]{0,1:T(8,128)S(1)}, f32[1408,128]{0,1:T(8,128)}, u32[]{:S(2)}) copy-start(f32[1408,128]{0,1:T(8,128)} %fusion.53) | copy-start | bytes 2162692
  182.6 6.0 %copy-start.10 = (f32[1408,128]{0,1:T(8,128)S(1)}, f32[1408,128]{0,1:T(8,128)}, u32[]{:S(2)}) copy-start(f32[1408,128]{0,1:T(8,128)} %convolution_multiply_fusion.3) | copy-start | bytes 2162692
  184.6 98.0 %collective-permute-start.2 = (bf16[2,384,384]{1,2,0:T(8,128)(2,1)}, bf16[2,384,384]{1,2,0:T(8,128)(2,1)}, u32[]{:S(2)}, u32[]{:S(2)}) collective-permute-start(bf16[2,384,384]{1,2,0:T(8,128)(2,1)} %pad_maximum_fusion.3), channel_id=1, source_target_pairs={{8,0},{16,8},{24,16},{32,24},{40,32},{48,40},{56,48},{9,1},{17,9},... | collective-permute-start | bytes 1769480 | tf_op jit(solution)/shard_map/ppermute | solution.py:45
  (35 other events, 85.0 us)
Sparse Core Ops, SparseCore 0:
  187.8 90.1 all-reduce.2
